TPU v7x, 32 devices: a whole 2x2x4 slice. The times are simulated.
32 devices in a mesh: row: 8 (over z, core), col: 4 (over y, x).
Axes of the slice: x: 2, y: 2, z: 4, core: 2. Of those that a mesh axis runs over, the one named last changes fastest.
Arguments:
- tensor: bfloat16 [512, 2048, 256], P(('row', 'col')), may hold values from -6 to 6
- factor_one: bfloat16 [512, 64], P(('row', 'col')), may hold values from -0.25 to 0.25
- factor_two: bfloat16 [2048, 64], P('col'), may hold values from -0.125 to 0.125
Outputs:
- gram: float32 [256, 256], replicated
All inputs are finite; a program needn't handle non-finite values.
Results may differ from a plain program's by a relative error of at most 0.0003.
Values may be sent and summed in bfloat16 or wider, within the bound.
A program may use at most 64 MiB of HBM per device.

v0:
```python
import functools

import jax
import jax.numpy as jnp
from jax import lax
from jax.experimental import pallas as pl
from jax.experimental.pallas import tpu as pltpu
from jax.sharding import PartitionSpec as P

MESH = pl.DeviceIdType.MESH
F32 = jnp.float32
BF16 = jnp.bfloat16
TILE = 8


def over_rows(left, right):
    return lax.dot_general(
        left, right, (((0,), (0,)), ((), ())), preferred_element_type=F32
    )


def split(x):
    high = x.astype(BF16)
    return high, (x - high.astype(F32)).astype(BF16)


def kernel(
    n_row, n_col, share,
    t_ref, f1_ref, f2_ref, out_ref,
    held, twos, ones, ones_all, spread, stage, recv, outbox, inbox, part, part_all, lines, total,
    load_sem, two_send, two_recv, one_send, one_recv,
    mid_send, mid_recv, box_send, box_recv, part_send, part_recv, line_send, line_recv, all_send, all_recv,
):
    slab, rank_one = f1_ref.shape
    rank_two = f2_ref.shape[0]
    chunks, depth = stage.shape[1], stage.shape[3]
    rows = slab * share
    per_chunk = slab // chunks
    my_row, my_col = lax.axis_index("row"), lax.axis_index("col")
    half_rows = n_row // 2
    n = half_rows * n_col
    my_half, my_seat = my_row // half_rows, lax.rem(my_row, half_rows)
    me = my_seat * n_col + my_col

    def place(d):
        return my_half * half_rows + d // n_col, lax.rem(d, n_col)


    def load(c):
        rows = pl.ds(c * per_chunk, per_chunk)
        return pltpu.make_async_copy(t_ref.at[rows], held.at[rows], load_sem.at[c])

    for c in range(chunks):
        load(c).start()

    barrier = pltpu.get_barrier_semaphore()

    def greet(off, _):
        d = lax.rem(my_row * n_col + my_col + off, 2 * n)
        pl.semaphore_signal(
            barrier, inc=1, device_id=(d // n_col, lax.rem(d, n_col)), device_id_type=MESH
        )
        return 0

    lax.fori_loop(1, 2 * n, greet, 0)

    iota = lambda shape, dim: lax.broadcasted_iota(jnp.int32, shape, dim)
    folds = slab // ones.shape[0]
    ones[...] = jnp.concatenate(
        [f1_ref[pl.ds(q * ones.shape[0], ones.shape[0]), :] for q in range(folds)], axis=1
    )
    ones_all[me] = ones[...]
    twos[my_col] = f2_ref[...]

    pl.semaphore_wait(barrier, 2 * n - 1)

    for off in range(1, n_col):
        pltpu.make_async_remote_copy(
            src_ref=f2_ref, dst_ref=twos.at[my_col],
            send_sem=two_send, recv_sem=two_recv,
            device_id=(my_row, lax.rem(my_col + off, n_col)), device_id_type=MESH,
        ).start()

    def to_all(src, dst, send_sem, recv_sem):
        def one(off, _):
            d = lax.rem(me + off, n)
            pltpu.make_async_remote_copy(
                src_ref=src(d), dst_ref=dst, send_sem=send_sem, recv_sem=recv_sem,
                device_id=place(d), device_id_type=MESH,
            ).start()
            return 0

        lax.fori_loop(1, n, one, 0)

    def wait_bytes(ref, sem):
        pltpu.make_async_copy(ref, ref, sem).wait()

    to_all(lambda d: ones, ones_all.at[me], one_send, one_recv)
    if n_col > 1:
        wait_bytes(twos.at[pl.ds(0, n_col - 1)], two_recv)
    second = jnp.concatenate([twos[q] for q in range(n_col)], axis=1)

    for c in range(chunks):
        load(c).wait()
        for i in range(per_chunk):
            partly = jnp.dot(second, held[c * per_chunk + i], preferred_element_type=F32)
            for b in range(rank_two // share):
                stage[b, c, pl.ds(i * share, share), :] = partly[b * share:(b + 1) * share, :]
        landing = recv.at[pl.ds(pl.multiple_of(me * rows + c * TILE, TILE), TILE)]
        to_all(lambda d: stage.at[d, c], landing, mid_send, mid_recv)

    recv[pl.ds(pl.multiple_of(me * rows, TILE), rows), :] = stage[me].reshape(rows, depth)
    wait_bytes(ones_all.at[pl.ds(0, n - 1)], one_recv)
    packed = ones_all[...].astype(F32)
    whole = jnp.concatenate(
        [packed[:, :, q * rank_one:(q + 1) * rank_one] for q in range(folds)], axis=1
    ).reshape(n * slab, rank_one)
    for j in range(share):
        for w in range(spread.shape[0]):
            parts = [
                whole if w * folds + p == j else jnp.zeros_like(whole) for p in range(folds)
            ]
            spread[w, pl.ds(j, n * slab, stride=share), :] = jnp.concatenate(parts, axis=1)
    first = jnp.concatenate([spread[w] for w in range(spread.shape[0])], axis=1).astype(BF16)
    wait_bytes(recv.at[pl.ds(0, (n - 1) * rows)], mid_recv)

    high, low = split(recv[...])
    flat = over_rows(first, high) + over_rows(first, low)
    outbox[...] = flat[:share * rank_one].reshape(outbox.shape)
    swap = pltpu.make_async_remote_copy(
        src_ref=outbox.at[1 - my_half], dst_ref=inbox, send_sem=box_send, recv_sem=box_recv,
        device_id=(lax.rem(my_row + half_rows, n_row), my_col), device_id_type=MESH,
    )
    swap.start()
    swap.wait_recv()
    flat = outbox[my_half] + inbox[...]
    high, low = split(flat)
    gram = over_rows(high, high) + over_rows(high, low) + over_rows(low, high)
    half = depth // 2
    part[...] = jnp.concatenate(
        [gram[:half, :half], gram[:half, half:], gram[half:, half:]], axis=0
    ).reshape(part.shape)

    plane, planes = part.shape[0], lines.shape[0]
    core, line = lax.rem(my_row, 2), my_row // 2
    seat = core * n_col + my_col

    def mate(off):
        other = lax.rem(seat + off, plane)
        return other, (line * 2 + other // n_col, lax.rem(other, n_col))

    def send(src, dst, send_sem, recv_sem, device):
        pltpu.make_async_remote_copy(
            src_ref=src, dst_ref=dst, send_sem=send_sem, recv_sem=recv_sem,
            device_id=device, device_id_type=MESH,
        ).start()

    for off in range(1, plane):
        other, device = mate(off)
        send(part.at[other], part_all.at[seat], part_send, part_recv, device)
    part_all[seat] = part[seat]
    wait_bytes(part_all.at[pl.ds(0, plane - 1)], part_recv)
    lines[line] = jnp.sum(part_all[...], axis=0)
    for off in range(1, planes):
        device = (lax.rem(line + off, planes) * 2 + core, my_col)
        send(lines.at[line], lines.at[line], line_send, line_recv, device)
    if planes > 1:
        wait_bytes(lines.at[pl.ds(0, planes - 1)], line_recv)
    total[seat] = jnp.sum(lines[...], axis=0)
    for off in range(1, plane):
        _, device = mate(off)
        send(total.at[seat], total.at[seat], all_send, all_recv, device)
    wait_bytes(total.at[pl.ds(0, plane - 1)], all_recv)

    blocks = total[...].reshape(3, half, half)
    out_ref[:half, :half] = blocks[0]
    out_ref[:half, half:] = blocks[1]
    out_ref[half:, :half] = blocks[1].T
    out_ref[half:, half:] = blocks[2]
    swap.wait_send()
    wait_bytes(part_all.at[pl.ds(0, plane - 1)], part_send)
    if planes > 1:
        wait_bytes(lines.at[pl.ds(0, planes - 1)], line_send)
    wait_bytes(total.at[pl.ds(0, plane - 1)], all_send)
    if n_col > 1:
        wait_bytes(twos.at[pl.ds(0, n_col - 1)], two_send)
    wait_bytes(ones_all.at[pl.ds(0, n - 1)], one_send)
    wait_bytes(recv.at[pl.ds(0, (n - 1) * rows)], mid_send)


def per_device(n_row, n_col, tensor, factor_one, factor_two):
    slab, second_size, depth = tensor.shape
    rank_one, rank_two = factor_one.shape[1], factor_two.shape[1]
    n = n_row // 2 * n_col
    share = rank_two // n
    plane, planes = 2 * n_col, n_row // 2
    half = depth // 2
    block = (3 * half // plane, half)
    chunks = slab * share // TILE
    packed = (slab * rank_one // 128, 128)
    dma = pltpu.SemaphoreType.DMA
    gram = pl.pallas_call(
        functools.partial(kernel, n_row, n_col, share),
        out_shape=jax.ShapeDtypeStruct((depth, depth), F32),
        in_specs=[
            pl.BlockSpec(memory_space=pl.ANY),
            pl.BlockSpec(memory_space=pltpu.VMEM),
            pl.BlockSpec(memory_space=pltpu.VMEM),
        ],
        out_specs=pl.BlockSpec(memory_space=pltpu.VMEM),
        scratch_shapes=[
            pltpu.VMEM(tensor.shape, BF16),
            pltpu.VMEM((n_col, rank_two, second_size // n_col), BF16),
            pltpu.VMEM(packed, BF16),
            pltpu.VMEM((n, *packed), BF16),
            pltpu.VMEM((-(-share * rank_one // 128), n * slab * share, 128), F32),
            pltpu.VMEM((rank_two // share, chunks, TILE, depth), F32),
            pltpu.VMEM((n * slab * share, depth), F32),
            pltpu.VMEM((2, share * rank_one // 2, depth), F32),
            pltpu.VMEM((share * rank_one // 2, depth), F32),
            pltpu.VMEM((plane, *block), F32),
            pltpu.VMEM((plane, *block), F32),
            pltpu.VMEM((planes, *block), F32),
            pltpu.VMEM((plane, *block), F32),
            dma((chunks,)),
        ] + [dma] * 14,
        compiler_params=pltpu.CompilerParams(
            collective_id=0, has_side_effects=True, vmem_limit_bytes=60 * 2**20
        ),
        name="project_and_gram",
    )(tensor, factor_one, factor_two.T)
    return gram / (rank_one * rank_two)


def solution(mesh):
    sizes = mesh.shape
    placed = (P(("row", "col"), None, None), P(("row", "col"), None), P("col", None))
    return jax.shard_map(
        functools.partial(per_device, sizes["row"], sizes["col"]),
        mesh=mesh, in_specs=placed, out_specs=P(), check_vma=False,
    )
```

profile of v0, /device:TPU:0, one launch (start us, length us, event | category | flops | bytes accessed | tf_op | source)
XLA Modules:
  0.0 50.1 jit_solution(14926685490004569261)
XLA Ops:
  0.0 48.4 %project_and_gram.1 = f32[256,256]{1,0:T(8,128)} custom-call(bf16[16,2048,256]{2,1,0:T(8,128)(2,1)} %t_ref.1, bf16[16,64]{1,0:T(8,128)(2,1)} %f1_ref.1, bf16[64,512]{1,0:T(8,128)(2,1)} %bitcast.1), custom_call_target="tpu_custom_call" | custom-call | tf_op jit(solution)/shard_map/project_and_gram/pallas_call | solution.py:202
  48.4 1.7 %broadcast_multiply_fusion = f32[256,256]{1,0:T(8,128)} fusion(f32[256,256]{1,0:T(8,128)} %project_and_gram.1), kind=kLoop, calls=%fused_computation | loop fusion | flops 65536 | bytes 524288 | tf_op jit(solution)/shard_map/div | solution.py:232
where the time goes:
time: 50.3 us; the launch traced here: 50.1 us
  Pallas kernels  48.4 us (96%)
  other arithmetic  1.67 us (3%)
    pallas_call x1, Pallas kernels, per_device(): pl.pallas_call(functools.partial(kernel, n_row, n_col, share), out_shape=...  48.4 us
    div x1, other arithmetic, per_device(): return gram / (rank_one * rank_two)  1.67 us

commit v1 on v0

v1 whole, which is shorter than its diff:
```python
import functools

import jax
import jax.numpy as jnp
from jax import lax
from jax.experimental import pallas as pl
from jax.experimental.pallas import tpu as pltpu
from jax.sharding import PartitionSpec as P

MESH = pl.DeviceIdType.MESH
F32 = jnp.float32
BF16 = jnp.bfloat16
LANES = 128
GROUP = 8
POWER = 5
TENSOR_LIMIT, ONE_LIMIT, TWO_LIMIT = 6.0, 0.25, 0.125


def split(x):
    high = x.astype(BF16)
    return high, (x - high.astype(F32)).astype(BF16)


def scale_for(bound):
    scale = 2.0 ** (125 // POWER)
    while bound > 1.0:
        bound, scale = bound / 2, scale / 2
    return scale


def dither(shape):
    places = lax.broadcasted_iota(jnp.int32, shape, 0) * 37 + lax.broadcasted_iota(jnp.int32, shape, 1) * 101
    return 1.0 + lax.rem(places, 128).astype(F32) * (2.0 ** -14 / POWER)


def encode(x, factor):
    x = x * factor
    square = x * x
    return (square * square * x).astype(BF16)


def decode(code, inverse):
    code = code.astype(F32)
    root = jnp.exp2(jnp.log2(jnp.abs(code)) * (1.0 / POWER)) * inverse
    return jnp.where(code < 0, -root, root)


def kernel(
    n_row, n_col, share,
    t_ref, f1_ref, f2_ref, out_ref,
    held, twos, ones, ones_all, spread, first, stage, sent, recv, outbox, inbox,
    part0, part1, part0_all, part1_all, total,
    load_sem, near_sem, two_send, two_recv, one_send, one_recv,
    mid_send, mid_recv, box_send, box_recv, part_send, part_recv, all_send, all_recv,
):
    slab, rank_one = f1_ref.shape
    rank_two, depth = f2_ref.shape[0], t_ref.shape[2]
    halves, chunks = sent.shape[0], sent.shape[1]
    rows = GROUP * share
    my_row, my_col = lax.axis_index("row"), lax.axis_index("col")
    half_rows = n_row // 2
    n = half_rows * n_col
    my_seat = lax.rem(my_row, half_rows)
    me = my_seat * n_col + my_col
    partner = (lax.rem(my_row + half_rows, n_row), my_col)
    pieces, block = part0.shape[0], part0.shape[1]

    for a in range(slab):
        pltpu.make_async_copy(t_ref.at[a], held.at[a], load_sem.at[a]).start()

    flips = []
    for i in range((n - 1).bit_length()):
        flips.append((1 - 2 * lax.rem(me // 2 ** i, 2)) * 2 ** i)

    def mates():
        for off in range(1, n):
            other = me
            for i, flip in enumerate(flips):
                if off >> i & 1:
                    other = other + flip
            col = lax.rem(other, n_col)
            yield other, (my_row - my_seat + (other - col) // n_col, col)

    def send(src, dst, send_sem, recv_sem, device):
        pltpu.make_async_remote_copy(
            src_ref=src, dst_ref=dst, send_sem=send_sem, recv_sem=recv_sem,
            device_id=device, device_id_type=MESH,
        ).start()

    def wait_bytes(ref, sem):
        pltpu.make_async_copy(ref, ref, sem).wait()

    cols = [(my_row, lax.rem(my_col + off, n_col)) for off in range(1, n_col)]
    lines = [(my_row - my_seat + lax.rem(my_seat + off, half_rows), my_col) for off in range(1, half_rows)]
    barrier = pltpu.get_barrier_semaphore()
    near = cols + lines + [partner]
    for device in near:
        pl.semaphore_signal(barrier, inc=1, device_id=device, device_id_type=MESH)
    twos[my_col] = f2_ref[...]
    folds = slab // GROUP
    ones[...] = jnp.concatenate([f1_ref[pl.ds(q * GROUP, GROUP), :] for q in range(folds)], axis=1)
    ones_all[me] = ones[...]
    pl.semaphore_wait(barrier, len(near))

    for device in cols:
        send(f2_ref, twos.at[my_col], two_send, two_recv, device)
    for device in lines:
        pl.semaphore_signal(near_sem, inc=1, device_id=device, device_id_type=MESH)
    factor = dither((rows, LANES))
    inverse = 1.0 / factor
    to_code = factor * scale_for(TENSOR_LIMIT * TWO_LIMIT * t_ref.shape[1])
    from_code = inverse * (1.0 / scale_for(TENSOR_LIMIT * TWO_LIMIT * t_ref.shape[1]))
    if lines:
        pl.semaphore_wait(near_sem, len(lines))
    for other, device in mates():
        send(ones, ones_all.at[me], one_send, one_recv, device)
    if cols:
        wait_bytes(twos.at[pl.ds(0, n_col - 1)], two_recv)
    second = jnp.concatenate([twos[q] for q in range(n_col)], axis=1)

    for h in range(halves):
        lanes = pl.ds(h * LANES, LANES)
        for c in range(chunks):
            for i in range(0, GROUP, 2):
                a = c * GROUP + i
                if h == 0:
                    for q in (a, a + 1):
                        pltpu.make_async_copy(t_ref.at[q], held.at[q], load_sem.at[q]).wait()
                pair = jnp.concatenate([held[a, :, lanes], held[a + 1, :, lanes]], axis=1)
                partly = jnp.dot(second, pair, preferred_element_type=F32)
                for q in range(2):
                    for b in range(n):
                        stage[b, pl.ds((i + q) * share, share), :] = partly[
                            b * share:(b + 1) * share, q * LANES:(q + 1) * LANES
                        ]
            for b in range(n):
                sent[h, c, b] = encode(stage[b], to_code)
            for other, device in mates():
                send(sent.at[h, c, other], recv.at[h, c, me], mid_send.at[h, c], mid_recv.at[h, c], device)
            recv[h, c, me] = sent[h, c, me]

    if n > 1:
        wait_bytes(ones_all.at[pl.ds(0, n - 1)], one_recv)
    packed = ones_all[...].astype(F32)
    words = spread.shape[0]
    for c in range(chunks):
        whole = packed[:, :, c * rank_one:(c + 1) * rank_one].reshape(n * GROUP, rank_one)
        per_word = LANES // rank_one
        for j in range(share):
            for w in range(words):
                cells = [whole if w * per_word + p == j else jnp.zeros_like(whole) for p in range(per_word)]
                spread[w, pl.ds(j, n * GROUP, stride=share), :] = jnp.concatenate(cells, axis=1)
        for w in range(words):
            first[c, pl.ds(w * LANES, LANES), :] = spread[w].T.astype(BF16)

    wide = dither((share * rank_one, LANES))
    core_scale = scale_for(TENSOR_LIMIT * TWO_LIMIT * t_ref.shape[1] * ONE_LIMIT * n * slab)
    core_to, core_from = wide * core_scale, (1.0 / wide) * (1.0 / core_scale)
    for h in range(halves):
        flat = None
        for c in range(chunks):
            wait_bytes(recv.at[h, c, pl.ds(0, n - 1)], mid_recv.at[h, c])
            value = decode(recv[h, c], from_code[None]).reshape(n * rows, LANES)
            high, low = split(value)
            both = jnp.dot(first[c], jnp.concatenate([high, low], axis=1), preferred_element_type=F32)
            both = both[:, :LANES] + both[:, LANES:]
            flat = both if flat is None else flat + both
        outbox[h] = encode(flat[:share * rank_one], core_to)
        send(outbox.at[h], inbox.at[h], box_send.at[h], box_recv.at[h], partner)

    mine = [decode(outbox[h], core_from) for h in range(halves)]
    turned, straight = [], []

    def product(i, j):
        (left_high, left_low), (right_high, right_low) = turned[i], straight[j]
        both = jnp.dot(left_high, jnp.concatenate([right_high, right_low], axis=1), preferred_element_type=F32)
        small = jnp.dot(left_low, right_high, preferred_element_type=F32)
        return (both[:, :LANES] + both[:, LANES:] + small).reshape(pieces, block, LANES)

    for h in range(halves):
        wait_bytes(inbox.at[h], box_recv.at[h])
        flat = mine[h] + decode(inbox[h], core_from)
        turned.append(split(flat.T))
        straight.append(split(flat))
        if h == 0:
            part0[...] = product(0, 0)
        else:
            part1[:, 0] = product(0, 1)
            part1[:, 1] = product(1, 1)
        source, landing = (part0, part0_all) if h == 0 else (part1, part1_all)
        for other, device in mates():
            @pl.when(other < pieces)
            def _():
                send(source.at[other], landing.at[me], part_send.at[h], part_recv.at[h], device)

    gain = 1.0 / (rank_one * rank_two)

    def finish():
        part0_all[me] = part0[me]
        part1_all[me] = part1[me]
        wait_bytes(part0_all.at[pl.ds(0, n - 1)], part_recv.at[0])
        total[me, 0] = jnp.sum(part0_all[...], axis=0) * gain
        wait_bytes(part1_all.at[pl.ds(0, n - 1)], part_recv.at[1])
        total[me, pl.ds(1, 2)] = jnp.sum(part1_all[...], axis=0) * gain
        for other, device in mates():
            send(total.at[me], total.at[me], all_send, all_recv, device)
        wait_bytes(part0.at[pl.ds(0, pieces - 1)], part_send.at[0])
        wait_bytes(part1.at[pl.ds(0, pieces - 1)], part_send.at[1])
        wait_bytes(total.at[pl.ds(0, pieces - 1)], all_recv)

    def follow():
        wait_bytes(part0, part_send.at[0])
        wait_bytes(part1, part_send.at[1])
        wait_bytes(total, all_recv)

    if n == pieces:
        finish()
    else:
        pl.when(me < pieces)(finish)
        pl.when(me >= pieces)(follow)

    blocks = [total[:, i].reshape(LANES, LANES) for i in range(3)]
    out_ref[:LANES, :LANES] = blocks[0]
    out_ref[:LANES, LANES:] = blocks[1]
    out_ref[LANES:, :LANES] = blocks[1].T
    out_ref[LANES:, LANES:] = blocks[2]

    if cols:
        wait_bytes(twos.at[pl.ds(0, n_col - 1)], two_send)
    wait_bytes(ones_all.at[pl.ds(0, n - 1)], one_send)
    for h in range(halves):
        for c in range(chunks):
            wait_bytes(recv.at[h, c, pl.ds(0, n - 1)], mid_send.at[h, c])
        wait_bytes(inbox.at[h], box_send.at[h])
    if n == pieces:
        wait_bytes(total.at[pl.ds(0, n - 1)], all_send)
    else:
        @pl.when(me < pieces)
        def _():
            wait_bytes(part0_all.at[pl.ds(0, n - 1)], all_send)
            wait_bytes(part1_all.at[pl.ds(0, n - 1)], all_send)


def per_device(n_row, n_col, tensor, factor_one, factor_two):
    slab, second_size, depth = tensor.shape
    rank_one, rank_two = factor_one.shape[1], factor_two.shape[1]
    n = n_row // 2 * n_col
    share = rank_two // n
    halves, chunks = depth // LANES, slab // GROUP
    rows = GROUP * share
    block = max(GROUP, LANES // n)
    pieces = LANES // block
    words = -(-share * rank_one // LANES)
    packed = (GROUP, slab // GROUP * rank_one)
    dma = pltpu.SemaphoreType.DMA
    gram = pl.pallas_call(
        functools.partial(kernel, n_row, n_col, share),
        out_shape=jax.ShapeDtypeStruct((depth, depth), F32),
        in_specs=[
            pl.BlockSpec(memory_space=pl.ANY),
            pl.BlockSpec(memory_space=pltpu.VMEM),
            pl.BlockSpec(memory_space=pltpu.VMEM),
        ],
        out_specs=pl.BlockSpec(memory_space=pltpu.VMEM),
        scratch_shapes=[
            pltpu.VMEM(tensor.shape, BF16),
            pltpu.VMEM((n_col, rank_two, second_size // n_col), BF16),
            pltpu.VMEM(packed, BF16),
            pltpu.VMEM((n, *packed), BF16),
            pltpu.VMEM((words, n * rows, LANES), F32),
            pltpu.VMEM((chunks, words * LANES, n * rows), BF16),
            pltpu.VMEM((n, rows, LANES), F32),
            pltpu.VMEM((halves, chunks, n, rows, LANES), BF16),
            pltpu.VMEM((halves, chunks, n, rows, LANES), BF16),
            pltpu.VMEM((halves, share * rank_one, LANES), BF16),
            pltpu.VMEM((halves, share * rank_one, LANES), BF16),
            pltpu.VMEM((pieces, block, LANES), F32),
            pltpu.VMEM((pieces, 2, block, LANES), F32),
            pltpu.VMEM((n, block, LANES), F32),
            pltpu.VMEM((n, 2, block, LANES), F32),
            pltpu.VMEM((pieces, 3, block, LANES), F32),
            dma((slab,)), pltpu.SemaphoreType.REGULAR,
            dma, dma, dma, dma, dma((halves, chunks)), dma((halves, chunks)),
            dma((halves,)), dma((halves,)), dma((halves,)), dma((halves,)), dma, dma,
        ],
        compiler_params=pltpu.CompilerParams(
            collective_id=0, has_side_effects=True, vmem_limit_bytes=60 * 2**20
        ),
        name="project_and_gram",
    )(tensor, factor_one, factor_two.T)
    return gram


def solution(mesh):
    sizes = mesh.shape
    placed = (P(("row", "col"), None, None), P(("row", "col"), None), P("col", None))
    return jax.shard_map(
        functools.partial(per_device, sizes["row"], sizes["col"]),
        mesh=mesh, in_specs=placed, out_specs=P(), check_vma=False,
    )
```

time: 50.3 us -> 39.7 us (0.79)
  Pallas kernels: 48.4 us -> 37.9 us
  other arithmetic: 1.67 us -> 0 us
  local copies, waits for them, and re-layouts: 0 us -> 1.67 us
    pallas_call x1, Pallas kernels: 48.4 us -> 37.9 us  [per_device(): pl.pallas_call(functools.partial(kernel, n_row, n_col, share), out_shape=...]
    div x1 -> x0, other arithmetic: 1.67 us -> none  [per_device(): return gram / (rank_one * rank_two)]
    unnamed x0 -> x1, local copies, waits for them, and re-layouts: none -> 1.67 us
where the time goes in v1:
time: 39.7 us; the launch traced here: 39.5 us
  Pallas kernels  37.9 us (95%)
  local copies, waits for them, and re-layouts  1.67 us (4%)
    pallas_call x1, Pallas kernels, per_device(): pl.pallas_call(functools.partial(kernel, n_row, n_col, share), out_shape=...  37.9 us
    unnamed x1, local copies, waits for them, and re-layouts  1.67 us

profile of v1, /device:TPU:0, one launch (start us, length us, event | category | flops | bytes accessed | tf_op | source)
XLA Modules:
  0.0 39.5 jit_solution(5133915396583750907)
XLA Ops:
  0.0 37.9 %project_and_gram.1 = f32[256,256]{1,0:T(8,128)} custom-call(bf16[16,2048,256]{2,1,0:T(8,128)(2,1)} %t_ref.1, bf16[16,64]{1,0:T(8,128)(2,1)} %f1_ref.1, bf16[64,512]{1,0:T(8,128)(2,1)} %bitcast.1), custom_call_target="tpu_custom_call" | custom-call | tf_op jit(solution)/shard_map/project_and_gram/pallas_call | solution.py:256
  37.9 1.7 %copy.5 = f32[256,256]{1,0:T(8,128)} copy(f32[256,256]{1,0:T(8,128)} %project_and_gram.1) | data formatting | bytes 524288

commit v2 on v1

--- a/solution.py
+++ b/solution.py
@@ -47,16 +47,16 @@
 
 def kernel(
     n_row, n_col, share,
-    t_ref, f1_ref, f2_ref, out_ref,
-    held, twos, ones, ones_all, spread, first, stage, sent, recv, outbox, inbox,
+    t_ref, f1_hbm, f2_hbm, out_ref,
+    held, f1_ref, twos, ones, ones_all, spread, first, stage, sent, recv, outbox, inbox,
     part0, part1, part0_all, part1_all, total,
-    load_sem, near_sem, two_send, two_recv, one_send, one_recv,
+    load_sem, small_sem, near_sem, two_send, two_recv, one_send, one_recv,
     mid_send, mid_recv, box_send, box_recv, part_send, part_recv, all_send, all_recv,
 ):
     slab, rank_one = f1_ref.shape
-    rank_two, depth = f2_ref.shape[0], t_ref.shape[2]
-    halves, chunks = sent.shape[0], sent.shape[1]
-    rows = GROUP * share
+    rank_two, depth = f2_hbm.shape[0], t_ref.shape[2]
+    halves, groups, chunks, _, rows, _ = sent.shape
+    each = share // groups
     my_row, my_col = lax.axis_index("row"), lax.axis_index("col")
     half_rows = n_row // 2
     n = half_rows * n_col
@@ -64,9 +64,6 @@
     me = my_seat * n_col + my_col
     partner = (lax.rem(my_row + half_rows, n_row), my_col)
     pieces, block = part0.shape[0], part0.shape[1]
-
-    for a in range(slab):
-        pltpu.make_async_copy(t_ref.at[a], held.at[a], load_sem.at[a]).start()
 
     flips = []
     for i in range((n - 1).bit_length()):
@@ -90,22 +87,29 @@
     def wait_bytes(ref, sem):
         pltpu.make_async_copy(ref, ref, sem).wait()
 
+    load_two = pltpu.make_async_copy(f2_hbm, twos.at[my_col], small_sem.at[0])
+    load_two.start()
     cols = [(my_row, lax.rem(my_col + off, n_col)) for off in range(1, n_col)]
     lines = [(my_row - my_seat + lax.rem(my_seat + off, half_rows), my_col) for off in range(1, half_rows)]
     barrier = pltpu.get_barrier_semaphore()
     near = cols + lines + [partner]
     for device in near:
         pl.semaphore_signal(barrier, inc=1, device_id=device, device_id_type=MESH)
-    twos[my_col] = f2_ref[...]
+    load_one = pltpu.make_async_copy(f1_hbm, f1_ref, small_sem.at[1])
+    load_one.start()
+    for a in range(slab):
+        pltpu.make_async_copy(t_ref.at[a], held.at[a], load_sem.at[a]).start()
+
+    load_two.wait()
+    pl.semaphore_wait(barrier, len(near))
+    for device in cols:
+        send(twos.at[my_col], twos.at[my_col], two_send, two_recv, device)
+    for device in lines:
+        pl.semaphore_signal(near_sem, inc=1, device_id=device, device_id_type=MESH)
+    load_one.wait()
     folds = slab // GROUP
     ones[...] = jnp.concatenate([f1_ref[pl.ds(q * GROUP, GROUP), :] for q in range(folds)], axis=1)
     ones_all[me] = ones[...]
-    pl.semaphore_wait(barrier, len(near))
-
-    for device in cols:
-        send(f2_ref, twos.at[my_col], two_send, two_recv, device)
-    for device in lines:
-        pl.semaphore_signal(near_sem, inc=1, device_id=device, device_id_type=MESH)
     factor = dither((rows, LANES))
     inverse = 1.0 / factor
     to_code = factor * scale_for(TENSOR_LIMIT * TWO_LIMIT * t_ref.shape[1])
@@ -117,6 +121,13 @@
     if cols:
         wait_bytes(twos.at[pl.ds(0, n_col - 1)], two_recv)
     second = jnp.concatenate([twos[q] for q in range(n_col)], axis=1)
+
+    def give(h, g, c):
+        for b in range(n):
+            sent[h, g, c, b] = encode(stage[g, c, b], to_code)
+        for other, device in mates():
+            send(sent.at[h, g, c, other], recv.at[h, g, c, me], mid_send.at[h, g, c], mid_recv.at[h, g, c], device)
+        recv[h, g, c, me] = sent[h, g, c, me]
 
     for h in range(halves):
         lanes = pl.ds(h * LANES, LANES)
@@ -130,45 +141,43 @@
                 partly = jnp.dot(second, pair, preferred_element_type=F32)
                 for q in range(2):
                     for b in range(n):
-                        stage[b, pl.ds((i + q) * share, share), :] = partly[
-                            b * share:(b + 1) * share, q * LANES:(q + 1) * LANES
-                        ]
-            for b in range(n):
-                sent[h, c, b] = encode(stage[b], to_code)
-            for other, device in mates():
-                send(sent.at[h, c, other], recv.at[h, c, me], mid_send.at[h, c], mid_recv.at[h, c], device)
-            recv[h, c, me] = sent[h, c, me]
+                        for g in range(groups):
+                            row = b * share + g * each
+                            stage[g, c, b, pl.ds((i + q) * each, each), :] = partly[
+                                row:row + each, q * LANES:(q + 1) * LANES
+                            ]
+            give(h, 0, c)
+        for g in range(1, groups):
+            for c in range(chunks):
+                give(h, g, c)
 
     if n > 1:
         wait_bytes(ones_all.at[pl.ds(0, n - 1)], one_recv)
     packed = ones_all[...].astype(F32)
-    words = spread.shape[0]
+    words, per_word, span = spread.shape[0], LANES // rank_one, n * GROUP * each
     for c in range(chunks):
         whole = packed[:, :, c * rank_one:(c + 1) * rank_one].reshape(n * GROUP, rank_one)
-        per_word = LANES // rank_one
-        for j in range(share):
+        for j in range(each):
             for w in range(words):
                 cells = [whole if w * per_word + p == j else jnp.zeros_like(whole) for p in range(per_word)]
-                spread[w, pl.ds(j, n * GROUP, stride=share), :] = jnp.concatenate(cells, axis=1)
-        for w in range(words):
-            first[c, pl.ds(w * LANES, LANES), :] = spread[w].T.astype(BF16)
-
-    wide = dither((share * rank_one, LANES))
+                spread[w, pl.ds(c * span + j, n * GROUP, stride=each), :] = jnp.concatenate(cells, axis=1)
+    for w in range(words):
+        first[pl.ds(w * LANES, LANES), :] = spread[w].T.astype(BF16)
+
+    wide = dither((each * rank_one, LANES))
     core_scale = scale_for(TENSOR_LIMIT * TWO_LIMIT * t_ref.shape[1] * ONE_LIMIT * n * slab)
     core_to, core_from = wide * core_scale, (1.0 / wide) * (1.0 / core_scale)
     for h in range(halves):
-        flat = None
-        for c in range(chunks):
-            wait_bytes(recv.at[h, c, pl.ds(0, n - 1)], mid_recv.at[h, c])
-            value = decode(recv[h, c], from_code[None]).reshape(n * rows, LANES)
-            high, low = split(value)
-            both = jnp.dot(first[c], jnp.concatenate([high, low], axis=1), preferred_element_type=F32)
-            both = both[:, :LANES] + both[:, LANES:]
-            flat = both if flat is None else flat + both
-        outbox[h] = encode(flat[:share * rank_one], core_to)
-        send(outbox.at[h], inbox.at[h], box_send.at[h], box_recv.at[h], partner)
-
-    mine = [decode(outbox[h], core_from) for h in range(halves)]
+        for g in range(groups):
+            for c in range(chunks):
+                wait_bytes(recv.at[h, g, c, pl.ds(0, n - 1)], mid_recv.at[h, g, c])
+            value = decode(recv[h, g].reshape(chunks * n, rows, LANES), from_code[None]).reshape(chunks * n * rows, LANES)
+            both = jnp.dot(first[...], jnp.concatenate(split(value), axis=1), preferred_element_type=F32)
+            core = (both[:, :LANES] + both[:, LANES:])[:each * rank_one]
+            outbox[h, g] = encode(core, core_to)
+            send(outbox.at[h, g], inbox.at[h, g], box_send.at[h, g], box_recv.at[h, g], partner)
+
+    mine = [[decode(outbox[h, g], core_from) for g in range(groups)] for h in range(halves)]
     turned, straight = [], []
 
     def product(i, j):
@@ -178,8 +187,11 @@
         return (both[:, :LANES] + both[:, LANES:] + small).reshape(pieces, block, LANES)
 
     for h in range(halves):
-        wait_bytes(inbox.at[h], box_recv.at[h])
-        flat = mine[h] + decode(inbox[h], core_from)
+        parts = []
+        for g in range(groups):
+            wait_bytes(inbox.at[h, g], box_recv.at[h, g])
+            parts.append(mine[h][g] + decode(inbox[h, g], core_from))
+        flat = jnp.concatenate(parts, axis=0)
         turned.append(split(flat.T))
         straight.append(split(flat))
         if h == 0:
@@ -229,9 +241,10 @@
         wait_bytes(twos.at[pl.ds(0, n_col - 1)], two_send)
     wait_bytes(ones_all.at[pl.ds(0, n - 1)], one_send)
     for h in range(halves):
-        for c in range(chunks):
-            wait_bytes(recv.at[h, c, pl.ds(0, n - 1)], mid_send.at[h, c])
-        wait_bytes(inbox.at[h], box_send.at[h])
+        for g in range(groups):
+            for c in range(chunks):
+                wait_bytes(recv.at[h, g, c, pl.ds(0, n - 1)], mid_send.at[h, g, c])
+            wait_bytes(inbox.at[h, g], box_send.at[h, g])
     if n == pieces:
         wait_bytes(total.at[pl.ds(0, n - 1)], all_send)
     else:
@@ -247,47 +260,50 @@
     n = n_row // 2 * n_col
     share = rank_two // n
     halves, chunks = depth // LANES, slab // GROUP
-    rows = GROUP * share
+    groups = 2 if share % 2 == 0 else 1
+    each = share // groups
+    rows = GROUP * each
     block = max(GROUP, LANES // n)
     pieces = LANES // block
-    words = -(-share * rank_one // LANES)
+    words = -(-each * rank_one // LANES)
     packed = (GROUP, slab // GROUP * rank_one)
     dma = pltpu.SemaphoreType.DMA
     gram = pl.pallas_call(
         functools.partial(kernel, n_row, n_col, share),
         out_shape=jax.ShapeDtypeStruct((depth, depth), F32),
         in_specs=[
-            pl.BlockSpec(memory_space=pl.ANY),
-            pl.BlockSpec(memory_space=pltpu.VMEM),
-            pl.BlockSpec(memory_space=pltpu.VMEM),
+            pl.BlockSpec(memory_space=pltpu.HBM),
+            pl.BlockSpec(memory_space=pltpu.HBM),
+            pl.BlockSpec(memory_space=pltpu.HBM),
         ],
         out_specs=pl.BlockSpec(memory_space=pltpu.VMEM),
         scratch_shapes=[
             pltpu.VMEM(tensor.shape, BF16),
+            pltpu.VMEM(factor_one.shape, BF16),
             pltpu.VMEM((n_col, rank_two, second_size // n_col), BF16),
             pltpu.VMEM(packed, BF16),
             pltpu.VMEM((n, *packed), BF16),
-            pltpu.VMEM((words, n * rows, LANES), F32),
-            pltpu.VMEM((chunks, words * LANES, n * rows), BF16),
-            pltpu.VMEM((n, rows, LANES), F32),
-            pltpu.VMEM((halves, chunks, n, rows, LANES), BF16),
-            pltpu.VMEM((halves, chunks, n, rows, LANES), BF16),
-            pltpu.VMEM((halves, share * rank_one, LANES), BF16),
-            pltpu.VMEM((halves, share * rank_one, LANES), BF16),
+            pltpu.VMEM((words, chunks * n * rows, LANES), F32),
+            pltpu.VMEM((words * LANES, chunks * n * rows), BF16),
+            pltpu.VMEM((groups, chunks, n, rows, LANES), F32),
+            pltpu.VMEM((halves, groups, chunks, n, rows, LANES), BF16),
+            pltpu.VMEM((halves, groups, chunks, n, rows, LANES), BF16),
+            pltpu.VMEM((halves, groups, each * rank_one, LANES), BF16),
+            pltpu.VMEM((halves, groups, each * rank_one, LANES), BF16),
             pltpu.VMEM((pieces, block, LANES), F32),
             pltpu.VMEM((pieces, 2, block, LANES), F32),
             pltpu.VMEM((n, block, LANES), F32),
             pltpu.VMEM((n, 2, block, LANES), F32),
             pltpu.VMEM((pieces, 3, block, LANES), F32),
-            dma((slab,)), pltpu.SemaphoreType.REGULAR,
-            dma, dma, dma, dma, dma((halves, chunks)), dma((halves, chunks)),
-            dma((halves,)), dma((halves,)), dma((halves,)), dma((halves,)), dma, dma,
+            dma((slab,)), dma((2,)), pltpu.SemaphoreType.REGULAR,
+            dma, dma, dma, dma, dma((halves, groups, chunks)), dma((halves, groups, chunks)),
+            dma((halves, groups)), dma((halves, groups)), dma((halves,)), dma((halves,)), dma, dma,
         ],
         compiler_params=pltpu.CompilerParams(
-            collective_id=0, has_side_effects=True, vmem_limit_bytes=60 * 2**20
+            collective_id=0, has_side_effects=True, vmem_limit_bytes=40 * 2**20
         ),
         name="project_and_gram",
-    )(tensor, factor_one, factor_two.T)
+    )(*(pltpu.with_memory_space_constraint(x, pltpu.HBM) for x in (tensor, factor_one, factor_two.T)))
     return gram
 
 

time: 39.7 us -> 36.1 us (0.909)
  Pallas kernels: 37.9 us -> 35.2 us
  local copies, waits for them, and re-layouts: 1.67 us -> 0.71 us
    pallas_call x1, Pallas kernels: 37.9 us -> 35.2 us  [per_device(): pl.pallas_call(functools.partial(kernel, n_row, n_col, share), out_shape=...]
    unnamed x1, local copies, waits for them, and re-layouts: 1.67 us -> 0.71 us
where the time goes in v2:
time: 36.1 us; the launch traced here: 36 us
  Pallas kernels  35.2 us (98%)
  local copies, waits for them, and re-layouts  0.71 us (2%)
    pallas_call x1, Pallas kernels, per_device(): pl.pallas_call(functools.partial(kernel, n_row, n_col, share), out_shape=...  35.2 us

profile of v2, /device:TPU:0, one launch (start us, length us, event | category | flops | bytes accessed | tf_op | source)
XLA Modules:
  0.0 36.0 jit_solution(711626482720376006)
XLA Ops:
  0.0 35.2 %project_and_gram.1 = f32[256,256]{1,0:T(8,128)S(1)} custom-call(bf16[16,2048,256]{2,1,0:T(8,128)(2,1)} %t_ref.1, bf16[16,64]{1,0:T(8,128)(2,1)} %f1_hbm.1, bf16[64,512]{1,0:T(8,128)(2,1)} %bitcast.1), custom_call_target="tpu_custom_call" | custom-call | tf_op jit(solution)/shard_map/project_and_gram/pallas_call | solution.py:271
  35.2 0.7 %copy.5 = f32[256,256]{1,0:T(8,128)} copy(f32[256,256]{1,0:T(8,128)S(1)} %project_and_gram.1) | data formatting | bytes 524288

commit v3 on v2

v3 whole, which is shorter than its diff:
```python
import functools

import jax
import jax.numpy as jnp
from jax import lax
from jax.experimental import pallas as pl
from jax.experimental.pallas import tpu as pltpu
from jax.sharding import PartitionSpec as P

MESH = pl.DeviceIdType.MESH
F32 = jnp.float32
BF16 = jnp.bfloat16
LANES = 128
GROUP = 8
POWER = 5
TENSOR_LIMIT, ONE_LIMIT, TWO_LIMIT = 6.0, 0.25, 0.125


def split(x):
    high = x.astype(BF16)
    return high, (x - high.astype(F32)).astype(BF16)


def scale_for(bound):
    scale = 2.0 ** (125 // POWER)
    while bound > 1.0:
        bound, scale = bound / 2, scale / 2
    return scale


def dither(shape):
    places = lax.broadcasted_iota(jnp.int32, shape, 0) * 37 + lax.broadcasted_iota(jnp.int32, shape, 1) * 101
    return 1.0 + lax.rem(places, 128).astype(F32) * (2.0 ** -14 / POWER)


def encode(x, factor):
    x = x * factor
    square = x * x
    return (square * square * x).astype(BF16)


def decode(code, inverse):
    code = code.astype(F32)
    root = jnp.exp2(jnp.log2(jnp.abs(code)) * (1.0 / POWER)) * inverse
    return jnp.where(code < 0, -root, root)


def kernel(
    n_row, n_col, share,
    t_ref, f1_hbm, f2_hbm, out_ref,
    held, f1_ref, twos, ones, ones_all, first, sums, stage, sent, recv, outbox, inbox,
    part0, part1, part0_all, part1_all, total,
    load_sem, small_sem, near_sem, two_send, two_recv, one_send, one_recv,
    mid_send, mid_recv, box_send, box_recv, part_send, part_recv, all_send, all_recv,
):
    slab, rank_one = f1_ref.shape
    rank_two, depth = f2_hbm.shape[0], t_ref.shape[2]
    halves, pairs, shard = sent.shape[0], slab // 2, f2_hbm.shape[1]
    my_row, my_col = lax.axis_index("row"), lax.axis_index("col")
    half_rows = n_row // 2
    n = half_rows * n_col
    my_half = my_row // half_rows
    base = my_half * half_rows
    other_core = lambda row: row + 1 - 2 * lax.rem(row, 2)
    crossed = lambda row: row + my_half * (1 - 2 * lax.rem(row, 2))
    me = crossed(my_row - base) * n_col + my_col
    partner = (other_core(lax.rem(my_row + half_rows, n_row)), my_col)
    pieces, block = part0.shape[0], part0.shape[1]

    def flipped(place, off):
        for i in range(off.bit_length()):
            if off >> i & 1:
                place = place + (1 - 2 * lax.rem(place // 2 ** i, 2)) * 2 ** i
        return place

    def mates():
        for off in sorted(range(1, n), key=lambda off: (-(off & ~n_col).bit_count(), off // n_col % 2)):
            other = flipped(me, off)
            col = lax.rem(other, n_col)
            yield other, (base + crossed((other - col) // n_col), col)

    def send(src, dst, send_sem, recv_sem, device):
        pltpu.make_async_remote_copy(
            src_ref=src, dst_ref=dst, send_sem=send_sem, recv_sem=recv_sem,
            device_id=device, device_id_type=MESH,
        ).start()

    def wait_bytes(ref, sem):
        pltpu.make_async_copy(ref, ref, sem).wait()

    load_two = pltpu.make_async_copy(f2_hbm, twos.at[my_col], small_sem.at[0])
    load_two.start()
    offs = sorted(range(1, n_col), key=lambda off: off.bit_count())
    cols = [(my_row, flipped(my_col, off)) for off in offs]
    lines = [(base + lax.rem(my_row - base + off, half_rows), my_col) for off in range(1, half_rows)]
    barrier = pltpu.get_barrier_semaphore()
    near = cols + lines + [partner]
    for device in near:
        pl.semaphore_signal(barrier, inc=1, device_id=device, device_id_type=MESH)
    load_one = pltpu.make_async_copy(f1_hbm, f1_ref, small_sem.at[1])
    load_one.start()
    def load(a):
        return pltpu.make_async_copy(t_ref.at[a], held.at[a], load_sem.at[a])

    for a in range(slab):
        load(a).start()

    load_two.wait()
    pl.semaphore_wait(barrier, len(near))
    for i, device in enumerate(cols):
        send(twos.at[my_col], twos.at[my_col], two_send, two_recv.at[i], device)
    for device in lines:
        pl.semaphore_signal(near_sem, inc=1, device_id=device, device_id_type=MESH)
    load_one.wait()
    folds = slab // GROUP
    ones[...] = jnp.concatenate([f1_ref[pl.ds(q * GROUP, GROUP), :] for q in range(folds)], axis=1)
    ones_all[me] = ones[...]
    factor = dither((slab, LANES))
    inverse = 1.0 / factor
    to_code = factor * scale_for(TENSOR_LIMIT * TWO_LIMIT * t_ref.shape[1])
    from_code = inverse * (1.0 / scale_for(TENSOR_LIMIT * TWO_LIMIT * t_ref.shape[1]))
    if lines:
        pl.semaphore_wait(near_sem, len(lines))
    for other, device in mates():
        send(ones, ones_all.at[me], one_send, one_recv, device)

    def place(h, p, partly):
        for q in range(2):
            stage[pl.ds(2 * p + q, rank_two, stride=slab), :] = partly[:, q * LANES:(q + 1) * LANES]

    def give(h):
        for g in range(share):
            for b in range(n):
                r = b * share + g
                sent[h, r] = encode(stage[pl.ds(r * slab, slab), :], to_code)
            for other, device in mates():
                send(sent.at[h, other * share + g], recv.at[h, g, me], mid_send.at[h, g], mid_recv.at[h, g], device)
            recv[h, g, me] = sent[h, me * share + g]

    def term(q, p):
        where = pl.ds(pl.multiple_of(q * shard, shard), shard)
        pair = jnp.concatenate([held[2 * p, where, :LANES], held[2 * p + 1, where, :LANES]], axis=1)
        return jnp.dot(twos[q], pair, preferred_element_type=F32)

    shards = [my_col] + [flipped(my_col, off) for off in offs]
    split_at = pairs // 2
    for some in (range(split_at), range(split_at, pairs)):
        for i, q in enumerate(shards[:-1]):
            if i and some[0] == 0:
                wait_bytes(twos.at[q], two_recv.at[i - 1])
            for p in some:
                if i == 0:
                    load(2 * p).wait()
                    load(2 * p + 1).wait()
                sums[p] = term(q, p) if i == 0 else sums[p] + term(q, p)
    wait_bytes(twos.at[shards[-1]], two_recv.at[len(shards) - 2])
    for p in range(pairs):
        place(0, p, sums[p] + term(shards[-1], p))
    give(0)
    second = jnp.concatenate([twos[q] for q in range(n_col)], axis=1)
    for h in range(1, halves):
        lanes = pl.ds(h * LANES, LANES)
        for p in range(pairs):
            pair = jnp.concatenate([held[2 * p, :, lanes], held[2 * p + 1, :, lanes]], axis=1)
            place(h, p, jnp.dot(second, pair, preferred_element_type=F32))
        give(h)

    if n > 1:
        wait_bytes(ones_all.at[pl.ds(0, n - 1)], one_recv)
    packed = ones_all[...].astype(F32)
    whole = jnp.concatenate(
        [packed[:, :, q * rank_one:(q + 1) * rank_one] for q in range(folds)], axis=1
    ).reshape(n * slab, rank_one)
    whole = jnp.concatenate([whole, jnp.zeros((n * slab, LANES - rank_one), F32)], axis=1)
    first[...] = whole.T[:rank_one].astype(BF16)

    wide = dither((rank_one, LANES))
    core_scale = scale_for(TENSOR_LIMIT * TWO_LIMIT * t_ref.shape[1] * ONE_LIMIT * n * slab)
    core_to, core_from = wide * core_scale, (1.0 / wide) * (1.0 / core_scale)
    for h in range(halves):
        for g in range(share):
            wait_bytes(recv.at[h, g, pl.ds(0, n - 1)], mid_recv.at[h, g])
            value = decode(recv[h, g], from_code[None]).reshape(n * slab, LANES)
            both = jnp.dot(first[...], jnp.concatenate(split(value), axis=1), preferred_element_type=F32)
            outbox[h, g] = encode(both[:, :LANES] + both[:, LANES:], core_to)
            send(outbox.at[h, g], inbox.at[h, g], box_send.at[h, g], box_recv.at[h, g], partner)

    mine = [[decode(outbox[h, g], core_from) for g in range(share)] for h in range(halves)]
    turned, straight = [], []

    def product(i, j):
        (left_high, left_low), (right_high, right_low) = turned[i], straight[j]
        both = jnp.dot(left_high, jnp.concatenate([right_high, right_low], axis=1), preferred_element_type=F32)
        small = jnp.dot(left_low, right_high, preferred_element_type=F32)
        return (both[:, :LANES] + both[:, LANES:] + small).reshape(pieces, block, LANES)

    for h in range(halves):
        parts = []
        for g in range(share):
            wait_bytes(inbox.at[h, g], box_recv.at[h, g])
            parts.append(mine[h][g] + decode(inbox[h, g], core_from))
        flat = jnp.concatenate(parts, axis=0)
        turned.append(split(flat.T))
        straight.append(split(flat))
        if h == 0:
            part0[...] = product(0, 0)
        else:
            part1[:, 0] = product(0, 1)
            part1[:, 1] = product(1, 1)
        source, landing = (part0, part0_all) if h == 0 else (part1, part1_all)
        for other, device in mates():
            @pl.when(other < pieces)
            def _():
                send(source.at[other], landing.at[me], part_send.at[h], part_recv.at[h], device)

    gain = 1.0 / (rank_one * rank_two)
    parts = ((part0, part0_all, pl.ds(0, 1)), (part1, part1_all, pl.ds(1, 2)))

    def finish():
        for i, (own, every, spot) in enumerate(parts):
            every[me] = own[me]
            wait_bytes(every.at[pl.ds(0, n - 1)], part_recv.at[i])
            total[me, spot] = (jnp.sum(every[...], axis=0) * gain).reshape(-1, block, LANES)
            for other, device in mates():
                send(total.at[me, spot], total.at[me, spot], all_send.at[i], all_recv.at[i], device)
        for i, (own, every, spot) in enumerate(parts):
            wait_bytes(own.at[pl.ds(0, pieces - 1)], part_send.at[i])
            wait_bytes(own.at[pl.ds(0, pieces - 1)], all_recv.at[i])

    def follow():
        for i, (own, every, spot) in enumerate(parts):
            wait_bytes(own, part_send.at[i])
            wait_bytes(own, all_recv.at[i])

    if n == pieces:
        finish()
    else:
        pl.when(me < pieces)(finish)
        pl.when(me >= pieces)(follow)

    blocks = [total[:, i].reshape(LANES, LANES) for i in range(3)]
    out_ref[:LANES, :LANES] = blocks[0]
    out_ref[:LANES, LANES:] = blocks[1]
    out_ref[LANES:, :LANES] = blocks[1].T
    out_ref[LANES:, LANES:] = blocks[2]

    if cols:
        wait_bytes(twos.at[pl.ds(0, n_col - 1)], two_send)
    wait_bytes(ones_all.at[pl.ds(0, n - 1)], one_send)
    for h in range(halves):
        for g in range(share):
            wait_bytes(recv.at[h, g, pl.ds(0, n - 1)], mid_send.at[h, g])
            wait_bytes(inbox.at[h, g], box_send.at[h, g])

    def leave():
        for i, (own, every, spot) in enumerate(parts):
            wait_bytes(every.at[pl.ds(0, n - 1)], all_send.at[i])

    if n == pieces:
        leave()
    else:
        pl.when(me < pieces)(leave)


def per_device(n_row, n_col, tensor, factor_one, factor_two):
    slab, second_size, depth = tensor.shape
    rank_one, rank_two = factor_one.shape[1], factor_two.shape[1]
    n = n_row // 2 * n_col
    share = rank_two // n
    halves = depth // LANES
    block = max(GROUP, LANES // n)
    pieces = LANES // block
    packed = (GROUP, slab // GROUP * rank_one)
    dma = pltpu.SemaphoreType.DMA
    gram = pl.pallas_call(
        functools.partial(kernel, n_row, n_col, share),
        out_shape=jax.ShapeDtypeStruct((depth, depth), F32),
        in_specs=[
            pl.BlockSpec(memory_space=pltpu.HBM),
            pl.BlockSpec(memory_space=pltpu.HBM),
            pl.BlockSpec(memory_space=pltpu.HBM),
        ],
        out_specs=pl.BlockSpec(memory_space=pltpu.VMEM),
        scratch_shapes=[
            pltpu.VMEM(tensor.shape, BF16),
            pltpu.VMEM(factor_one.shape, BF16),
            pltpu.VMEM((n_col, rank_two, second_size // n_col), BF16),
            pltpu.VMEM(packed, BF16),
            pltpu.VMEM((n, *packed), BF16),
            pltpu.VMEM((rank_one, n * slab), BF16),
            pltpu.VMEM((slab // 2, rank_two, 2 * LANES), F32),
            pltpu.VMEM((rank_two * slab, LANES), F32),
            pltpu.VMEM((halves, rank_two, slab, LANES), BF16),
            pltpu.VMEM((halves, share, n, slab, LANES), BF16),
            pltpu.VMEM((halves, share, rank_one, LANES), BF16),
            pltpu.VMEM((halves, share, rank_one, LANES), BF16),
            pltpu.VMEM((pieces, block, LANES), F32),
            pltpu.VMEM((pieces, 2, block, LANES), F32),
            pltpu.VMEM((n, block, LANES), F32),
            pltpu.VMEM((n, 2, block, LANES), F32),
            pltpu.VMEM((pieces, 3, block, LANES), F32),
            dma((slab,)), dma((2,)), pltpu.SemaphoreType.REGULAR,
            dma, dma((n_col,)), dma, dma, dma((halves, share)), dma((halves, share)),
            dma((halves, share)), dma((halves, share)), dma((halves,)), dma((halves,)), dma((halves,)), dma((halves,)),
        ],
        compiler_params=pltpu.CompilerParams(
            collective_id=0, has_side_effects=True, vmem_limit_bytes=40 * 2**20
        ),
        name="project_and_gram",
    )(*(pltpu.with_memory_space_constraint(x, pltpu.HBM) for x in (tensor, factor_one, factor_two.T)))
    return gram


def solution(mesh):
    sizes = mesh.shape
    placed = (P(("row", "col"), None, None), P(("row", "col"), None), P("col", None))
    return jax.shard_map(
        functools.partial(per_device, sizes["row"], sizes["col"]),
        mesh=mesh, in_specs=placed, out_specs=P(), check_vma=False,
    )
```

time: 36.1 us -> 33.1 us (0.917)
  Pallas kernels: 35.2 us -> 32.3 us
    pallas_call x1, Pallas kernels: 35.2 us -> 32.3 us  [per_device(): pl.pallas_call(functools.partial(kernel, n_row, n_col, share), out_shape=...]
where the time goes in v3:
time: 33.1 us; the launch traced here: 33 us
  Pallas kernels  32.3 us (98%)
  local copies, waits for them, and re-layouts  0.71 us (2%)
    pallas_call x1, Pallas kernels, per_device(): pl.pallas_call(functools.partial(kernel, n_row, n_col, share), out_shape=...  32.3 us
    unnamed x1, local copies, waits for them, and re-layouts  0.71 us

profile of v3, /device:TPU:0, one launch (start us, length us, event | category | flops | bytes accessed | tf_op | source)
XLA Modules:
  0.0 33.0 jit_solution(9750974066410046742)
XLA Ops:
  0.0 32.3 %project_and_gram.1 = f32[256,256]{1,0:T(8,128)S(1)} custom-call(bf16[16,2048,256]{2,1,0:T(8,128)(2,1)} %t_ref.1, bf16[16,64]{1,0:T(8,128)(2,1)} %f1_hbm.1, bf16[64,512]{1,0:T(8,128)(2,1)} %bitcast.1), custom_call_target="tpu_custom_call" | custom-call | tf_op jit(solution)/shard_map/project_and_gram/pallas_call | solution.py:275
  32.3 0.7 %copy.5 = f32[256,256]{1,0:T(8,128)} copy(f32[256,256]{1,0:T(8,128)S(1)} %project_and_gram.1) | data formatting | bytes 524288

commit v4 on v3

--- a/solution.py
+++ b/solution.py
@@ -99,16 +99,19 @@
         pl.semaphore_signal(barrier, inc=1, device_id=device, device_id_type=MESH)
     load_one = pltpu.make_async_copy(f1_hbm, f1_ref, small_sem.at[1])
     load_one.start()
-    def load(a):
-        return pltpu.make_async_copy(t_ref.at[a], held.at[a], load_sem.at[a])
-
-    for a in range(slab):
-        load(a).start()
+    def load(p):
+        two = pl.ds(2 * p, 2)
+        return pltpu.make_async_copy(t_ref.at[two], held.at[two], load_sem.at[p])
+
+    for p in range(2):
+        load(p).start()
 
     load_two.wait()
     pl.semaphore_wait(barrier, len(near))
     for i, device in enumerate(cols):
         send(twos.at[my_col], twos.at[my_col], two_send, two_recv.at[i], device)
+    for p in range(2, pairs):
+        load(p).start()
     for device in lines:
         pl.semaphore_signal(near_sem, inc=1, device_id=device, device_id_type=MESH)
     load_one.wait()
@@ -143,15 +146,14 @@
         return jnp.dot(twos[q], pair, preferred_element_type=F32)
 
     shards = [my_col] + [flipped(my_col, off) for off in offs]
-    split_at = pairs // 2
+    split_at = pairs * 3 // 4
     for some in (range(split_at), range(split_at, pairs)):
         for i, q in enumerate(shards[:-1]):
             if i and some[0] == 0:
                 wait_bytes(twos.at[q], two_recv.at[i - 1])
             for p in some:
                 if i == 0:
-                    load(2 * p).wait()
-                    load(2 * p + 1).wait()
+                    load(p).wait()
                 sums[p] = term(q, p) if i == 0 else sums[p] + term(q, p)
     wait_bytes(twos.at[shards[-1]], two_recv.at[len(shards) - 2])
     for p in range(pairs):

time: 33.1 us -> 32.8 us (level)
  no operation moved by 1% of the time
where the time goes in v4:
time: 32.8 us; the launch traced here: 32.7 us
  Pallas kernels  32 us (98%)
  local copies, waits for them, and re-layouts  0.71 us (2%)
    pallas_call x1, Pallas kernels, per_device(): pl.pallas_call(functools.partial(kernel, n_row, n_col, share), out_shape=...  32 us
    unnamed x1, local copies, waits for them, and re-layouts  0.71 us

profile of v4, /device:TPU:0, one launch (start us, length us, event | category | flops | bytes accessed | tf_op | source)
XLA Modules:
  0.0 32.7 jit_solution(15130438471670118053)
XLA Ops:
  0.0 32.0 %project_and_gram.1 = f32[256,256]{1,0:T(8,128)S(1)} custom-call(bf16[16,2048,256]{2,1,0:T(8,128)(2,1)} %t_ref.1, bf16[16,64]{1,0:T(8,128)(2,1)} %f1_hbm.1, bf16[64,512]{1,0:T(8,128)(2,1)} %bitcast.1), custom_call_target="tpu_custom_call" | custom-call | tf_op jit(solution)/shard_map/project_and_gram/pallas_call | solution.py:277
  32.0 0.7 %copy.5 = f32[256,256]{1,0:T(8,128)} copy(f32[256,256]{1,0:T(8,128)S(1)} %project_and_gram.1) | data formatting | bytes 524288

commit v5 on v4

--- a/solution.py
+++ b/solution.py
@@ -62,9 +62,9 @@
     my_half = my_row // half_rows
     base = my_half * half_rows
     other_core = lambda row: row + 1 - 2 * lax.rem(row, 2)
-    crossed = lambda row: row + my_half * (1 - 2 * lax.rem(row, 2))
+    crossed = lambda row: row + my_half * (half_rows - 1 - 2 * row)
     me = crossed(my_row - base) * n_col + my_col
-    partner = (other_core(lax.rem(my_row + half_rows, n_row)), my_col)
+    partner = (n_row - 1 - my_row, my_col)
     pieces, block = part0.shape[0], part0.shape[1]
 
     def flipped(place, off):

time: 32.8 us -> 32.3 us (0.985)
  Pallas kernels: 32 us -> 31.5 us
    pallas_call x1, Pallas kernels: 32 us -> 31.5 us  [per_device(): pl.pallas_call(functools.partial(kernel, n_row, n_col, share), out_shape=...]
where the time goes in v5:
time: 32.3 us; the launch traced here: 32.2 us
  Pallas kernels  31.5 us (98%)
  local copies, waits for them, and re-layouts  0.71 us (2%)
    pallas_call x1, Pallas kernels, per_device(): pl.pallas_call(functools.partial(kernel, n_row, n_col, share), out_shape=...  31.5 us
    unnamed x1, local copies, waits for them, and re-layouts  0.71 us

profile of v5, /device:TPU:0, one launch (start us, length us, event | category | flops | bytes accessed | tf_op | source)
XLA Modules:
  0.0 32.2 jit_solution(14339803834406504579)
XLA Ops:
  0.0 31.5 %project_and_gram.1 = f32[256,256]{1,0:T(8,128)S(1)} custom-call(bf16[16,2048,256]{2,1,0:T(8,128)(2,1)} %t_ref.1, bf16[16,64]{1,0:T(8,128)(2,1)} %f1_hbm.1, bf16[64,512]{1,0:T(8,128)(2,1)} %bitcast.1), custom_call_target="tpu_custom_call" | custom-call | tf_op jit(solution)/shard_map/project_and_gram/pallas_call | solution.py:277
  31.5 0.7 %copy.5 = f32[256,256]{1,0:T(8,128)} copy(f32[256,256]{1,0:T(8,128)S(1)} %project_and_gram.1) | data formatting | bytes 524288

commit v6 on v5

--- a/solution.py
+++ b/solution.py
@@ -74,7 +74,7 @@
         return place
 
     def mates():
-        for off in sorted(range(1, n), key=lambda off: (-(off & ~n_col).bit_count(), off // n_col % 2)):
+        for off in sorted(range(1, n), key=lambda off: (-(off & ~n_col).bit_count(), 1 - off // n_col % 2)):
             other = flipped(me, off)
             col = lax.rem(other, n_col)
             yield other, (base + crossed((other - col) // n_col), col)
@@ -103,14 +103,14 @@
         two = pl.ds(2 * p, 2)
         return pltpu.make_async_copy(t_ref.at[two], held.at[two], load_sem.at[p])
 
-    for p in range(2):
+    for p in range(4):
         load(p).start()
 
     load_two.wait()
     pl.semaphore_wait(barrier, len(near))
     for i, device in enumerate(cols):
         send(twos.at[my_col], twos.at[my_col], two_send, two_recv.at[i], device)
-    for p in range(2, pairs):
+    for p in range(4, pairs):
         load(p).start()
     for device in lines:
         pl.semaphore_signal(near_sem, inc=1, device_id=device, device_id_type=MESH)

time: 32.3 us -> 32.1 us (level)
  no operation moved by 1% of the time
where the time goes in v6:
time: 32.1 us; the launch traced here: 32 us
  Pallas kernels  31.3 us (98%)
  local copies, waits for them, and re-layouts  0.71 us (2%)
    pallas_call x1, Pallas kernels, per_device(): pl.pallas_call(functools.partial(kernel, n_row, n_col, share), out_shape=...  31.3 us
    unnamed x1, local copies, waits for them, and re-layouts  0.71 us

profile of v6, /device:TPU:0, one launch (start us, length us, event | category | flops | bytes accessed | tf_op | source)
XLA Modules:
  0.0 32.0 jit_solution(13410223991721561137)
XLA Ops:
  0.0 31.3 %project_and_gram.1 = f32[256,256]{1,0:T(8,128)S(1)} custom-call(bf16[16,2048,256]{2,1,0:T(8,128)(2,1)} %t_ref.1, bf16[16,64]{1,0:T(8,128)(2,1)} %f1_hbm.1, bf16[64,512]{1,0:T(8,128)(2,1)} %bitcast.1), custom_call_target="tpu_custom_call" | custom-call | tf_op jit(solution)/shard_map/project_and_gram/pallas_call | solution.py:277
  31.3 0.7 %copy.5 = f32[256,256]{1,0:T(8,128)} copy(f32[256,256]{1,0:T(8,128)S(1)} %project_and_gram.1) | data formatting | bytes 524288
